TPU v7x, 32 devices: a whole 2x2x4 slice. The times are simulated.
32 devices in a mesh: dp: 4 (over y, core), mp: 8 (over z, x).
Axes of the slice: x: 2, y: 2, z: 4, core: 2. Of those that a mesh axis runs over, the one named last changes fastest.
Arguments:
- layer_input: bfloat16 [128, 256, 768], P(('dp', 'mp')), may hold values from -6 to 6
- output_cot: bfloat16 [128, 256, 768], P(('dp', 'mp')), may hold values from -6 to 6
- hidden_act: bfloat16 [128, 3072, 256], P('dp', 'mp'), may hold values from 0 to 2
- hidden_cot: bfloat16 [128, 3072, 256], P('dp', 'mp'), may hold values from -6 to 6
- lengths: int32 [128], P('dp'), may hold values from 32 to 256
- weights: float32 [768, 6144], P('dp', 'mp'), may hold values from -0.21875 to 0.21875
- moment_one: float32 [768, 6144], P('dp', 'mp'), may hold values from -3 to 3
- moment_two: float32 [768, 6144], P('dp', 'mp'), may hold values from 0.0005 to 0.02
Outputs:
- new_weights: float32 [768, 6144], P('dp', 'mp')
- new_moment_one: float32 [768, 6144], P('dp', 'mp')
- new_moment_two: float32 [768, 6144], P('dp', 'mp')
- clip_scale: float32 [128], P('dp')
Inputs may be any that keep to these rules, and one draw needn't show every extreme that they name: `lengths`: slots from an example's length on are padding.
All inputs are finite; a program needn't handle non-finite values.
Results may differ from a plain program's by a relative error of at most 0.0024.
Values may be sent and summed in bfloat16 or wider, within the bound.
A program may use at most 128 MiB of HBM per device.

v0:
```python
import math
import jax
import jax.numpy as jnp
from jax import lax
from jax.sharding import PartitionSpec as P

D = 768
FF = 3072
SLOT = 256
STEP = 10
beta_one = 0.9
beta_two = 0.999
adam_eps = 1e-08
learn_rate = 0.001
weight_decay = 0.01


def squared_norms(input_rows, outcot_rows, cot_rows, hid_rows):
    input_gram = jnp.einsum(
        "esd,etd->est", input_rows, input_rows, preferred_element_type=jnp.float32
    )
    cot_gram = jnp.einsum("efs,eft->est", cot_rows, cot_rows, preferred_element_type=jnp.float32)
    outcot_gram = jnp.einsum(
        "esd,etd->est", outcot_rows, outcot_rows, preferred_element_type=jnp.float32
    )
    hid_gram = jnp.einsum("efs,eft->est", hid_rows, hid_rows, preferred_element_type=jnp.float32)
    return jnp.sum(input_gram * cot_gram + outcot_gram * hid_gram, axis=(1, 2))


def clip_factor(squares):
    clip_limit = 0.5 * math.sqrt(2.0 * D * FF * SLOT)
    return clip_limit / jnp.maximum(jnp.sqrt(squares), clip_limit)


def masked_rows(own_lengths, hidden_cot, hidden_act):
    slot_index = lax.broadcasted_iota(jnp.int32, (own_lengths.shape[0], SLOT), 1)
    token_mask = (slot_index < own_lengths[:, None]).astype(jnp.float32)
    cot_masked = (hidden_cot.astype(jnp.float32) * token_mask[:, None, :]).astype(jnp.bfloat16)
    hid_masked = (hidden_act.astype(jnp.float32) * token_mask[:, None, :]).astype(jnp.bfloat16)
    return (token_mask, cot_masked, hid_masked)


def scaled_rows(clip_scale, token_mask, hidden_cot, hidden_act):
    factor = clip_scale[:, None] * token_mask
    scaled_cot = (hidden_cot.astype(jnp.float32) * factor[:, None, :]).astype(jnp.bfloat16)
    scaled_hid = (hidden_act.astype(jnp.float32) * factor[:, None, :]).astype(jnp.bfloat16)
    return (scaled_cot, scaled_hid)


def gradient_rows(input_rows, outcot_rows, cot_rows, hid_rows, row_count):
    contract = (((0, 1), (0, 2)), ((), ()))
    first_part = lax.dot_general(input_rows, cot_rows, contract, preferred_element_type=jnp.float32)
    second_part = lax.dot_general(
        outcot_rows, hid_rows, contract, preferred_element_type=jnp.float32
    )
    unit_count = cot_rows.shape[1]
    return jnp.stack([first_part, second_part], axis=2).reshape(row_count, 2 * unit_count)


def local(
    layer_input, output_cot, hidden_act, hidden_cot, lengths, weights, moment_one, moment_two
):
    local_examples = lengths.shape[0]
    input_full, outcot_full = (
        lax.all_gather(layer_input, "mp", axis=0, tiled=True),
        lax.all_gather(output_cot, "mp", axis=0, tiled=True),
    )
    token_mask, cot_masked, hid_masked = masked_rows(lengths, hidden_cot, hidden_act)
    partial_squares = squared_norms(input_full, outcot_full, cot_masked, hid_masked)
    squares = lax.psum(partial_squares, "mp")
    clip_scale = clip_factor(squares)
    scaled_cot, scaled_hid = scaled_rows(clip_scale, token_mask, hidden_cot, hidden_act)
    summed = lax.psum_scatter(
        gradient_rows(
            input_full,
            outcot_full,
            scaled_cot,
            scaled_hid,
            D // lax.axis_size("dp") * lax.axis_size("dp"),
        ).astype(jnp.bfloat16),
        "dp",
        scatter_dimension=0,
        tiled=True,
    ).astype(jnp.float32)
    gradient = summed / (local_examples * lax.axis_size("dp"))
    new_moment_one = beta_one * moment_one + (1.0 - beta_one) * gradient
    new_moment_two = beta_two * moment_two + (1.0 - beta_two) * gradient * gradient
    corr_one = 1.0 - beta_one**STEP
    corr_two = 1.0 - beta_two**STEP
    direction = new_moment_one / corr_one / (jnp.sqrt(new_moment_two / corr_two) + adam_eps)
    new_weights = weights - learn_rate * (direction + weight_decay * weights)
    return (new_weights, new_moment_one, new_moment_two, clip_scale)


def solution(mesh):
    return jax.shard_map(
        local,
        mesh=mesh,
        in_specs=(
            P(("dp", "mp"), None, None),
            P(("dp", "mp"), None, None),
            P("dp", "mp", None),
            P("dp", "mp", None),
            P("dp"),
            P("dp", "mp"),
            P("dp", "mp"),
            P("dp", "mp"),
        ),
        out_specs=(P("dp", "mp"), P("dp", "mp"), P("dp", "mp"), P("dp")),
        check_vma=False,
    )
```

profile of v0, /device:TPU:0, one launch (start us, length us, event | category | flops | bytes accessed | tf_op | source)
XLA Modules:
  0.0 470.0 jit_solution(956524610388416059)
XLA Ops:
  7.2 0.0 all-gather.5.cloned.1.call-start
  7.2 0.7 all-gather.5.cloned.1.call-update
  7.9 0.0 all-gather.3.cloned.1.call-start
  7.9 0.7 all-gather.3.cloned.1.call-update
  8.6 0.0 reduce-scatter.4.cloned.1.call-start
  8.7 0.7 fusion.40
  9.4 10.9 %fusion.6 = f32[32,256,256]{2,1,0:T(8,128)} fusion(bf16[32,384,256]{2,1,0:T(8,128)(2,1)} %param.10, f32[32,256]{1,0:T(8,128)S(1)} %fusion.40), kind=kOutput, calls=%fused_computation.10 | convolution fusion | flops 1620049920 | bytes 14712832 | tf_op jit(solution)/shard_map/efs,eft->est/dot_general | solution.py:26
  20.3 168.7 %all-gather.5.cloned.1.call-done = bf16[32,256,768]{2,1,0:T(8,128)(2,1)} async-done(((bf16[4,256,768]{2,1,0:T(8,128)(2,1)}), bf16[32,256,768]{2,1,0:T(8,128)(2,1)}) %all-gather.5.cloned.1.call-update) | async-done | bytes 12582928 | tf_op jit(solution)/shard_map/all_gather | solution.py:66
  189.0 16.7 %fusion.44 = f32[32,256,256]{2,1,0:T(8,128)} fusion(bf16[32,256,768]{2,1,0:T(8,128)(2,1)} %all-gather.5.cloned.1.call-done), kind=kOutput, calls=%fused_computation.36 | convolution fusion | flops 3221225472 | bytes 20971520 | tf_op jit(solution)/shard_map/esd,etd->est/dot_general | solution.py:23
  205.7 159.8 %all-gather.3.cloned.1.call-done = bf16[32,256,768]{2,1,0:T(8,128)(2,1)} async-done(((bf16[4,256,768]{2,1,0:T(8,128)(2,1)}), bf16[32,256,768]{2,1,0:T(8,128)(2,1)}) %all-gather.3.cloned.1.call-update) | async-done | bytes 12582928 | tf_op jit(solution)/shard_map/all_gather | solution.py:65
  365.5 16.5 %fusion.43 = f32[32,256,256]{2,1,0:T(8,128)} fusion(bf16[32,256,768]{2,1,0:T(8,128)(2,1)} %all-gather.3.cloned.1.call-done), kind=kOutput, calls=%fused_computation.35 | convolution fusion | flops 3221225472 | bytes 20971520 | tf_op jit(solution)/shard_map/esd,etd->est/dot_general | solution.py:19
  382.0 14.5 %add_reduce_fusion = f32[32]{0:T(128)S(1)} fusion(f32[32,256,256]{2,1,0:T(8,128)} %fusion.44, f32[32,256,256]{2,1,0:T(8,128)} %fusion.6, f32[32,256,256]{2,1,0:T(8,128)} %fusion.43, bf16[32,384,256]{2,1,0:T(8,128)(2,1)} %param.11, f32[32,256]{1,0:T(8,128)S(1)} %fusion.40), kind=kOutput, calls=%fused_computation.8 | convolution fusion | flops 1628438528 | bytes 31490176 | tf_op jit(solution)/shard_map/efs,eft->est/dot_general | solution.py:22
  396.5 18.7 %psum.7 = f32[32]{0:T(128)S(1)} all-reduce(f32[32]{0:T(128)S(1)} %add_reduce_fusion), channel_id=1, replica_groups=mesh['dp'=4,'mp'=8] {'mp'}, use_global_device_ids=true, to_apply=%region_1.0 | all-reduce | flops 32 | bytes 256 | tf_op jit(solution)/shard_map/psum | solution.py:70
  415.3 0.0 copy-done.2
  415.3 0.0 copy-start.3
  415.3 0.1 fusion.39
  415.3 11.0 %fusion.33 = bf16[768,384,1]{0,1,2:T(8,128)(2,1)S(1)} fusion(bf16[32,256,768]{2,1,0:T(8,128)(2,1)} %all-gather.5.cloned.1.call-done, bf16[32,384,256]{2,1,0:T(8,128)(2,1)} %param.10, f32[32,256]{1,0:T(8,128)S(1)} %fusion.39), kind=kOutput, calls=%fused_computation.22 | convolution fusion | flops 4841570304 | bytes 19496960 | tf_op jit(solution)/shard_map/dot_general | solution.py:53
  426.3 0.0 copy-done.3
  426.3 0.0 slice-done
  426.4 0.0 slice-done.1
  426.4 8.1 %fusion.30 = bf16[768,384,1]{0,1,2:T(8,128)(2,1)S(1)} fusion(bf16[32,256,768]{2,1,0:T(8,128)(2,1)} %all-gather.3.cloned.1.call-done, bf16[32,384,256]{2,1,0:T(8,128)(2,1)S(1)} %bitcast.30, f32[32,256]{1,0:T(8,128)S(1)} %fusion.39), kind=kOutput, calls=%fused_computation.21 | convolution fusion | flops 4841570304 | bytes 19496960 | tf_op jit(solution)/shard_map/dot_general | solution.py:52
  434.5 0.0 copy-start
  434.5 0.0 copy-start.1
  434.5 0.1 pad_maximum_fusion
  434.6 1.2 copy.36
  435.8 0.5 convert_element_type.41
  436.3 1.5 copy.40
  437.8 0.0 reduce-scatter.4.cloned.1.call-update
  437.8 23.0 %reduce-scatter.4.cloned.1.call-done = bf16[192,768]{1,0:T(8,128)(2,1)} async-done(((bf16[768,768]{1,0:T(8,128)(2,1)}), bf16[192,768]{1,0:T(8,128)(2,1)}) %reduce-scatter.4.cloned.1.call-update) | async-done | bytes 294928 | tf_op jit(solution)/shard_map/reduce_scatter | solution.py:73
  460.8 0.0 copy-done
  460.8 0.0 copy-done.1
  460.8 2.7 multiply_subtract_fusion
  (5 shorter events, 0.0 us)
Async XLA Ops:
  7.2 181.8 %all-gather.5.cloned.1.call-start = ((), (), s32[]{:S(2)}) async-start(), calls=%async_computation.2 | async-start | bytes 14155776 | tf_op jit(solution)/shard_map/all_gather | solution.py:66
  7.9 357.6 %all-gather.3.cloned.1.call-start = ((), (), s32[]{:S(2)}) async-start(), calls=%async_computation.1 | async-start | bytes 14155776 | tf_op jit(solution)/shard_map/all_gather | solution.py:65
  8.6 452.2 %reduce-scatter.4.cloned.1.call-start = ((), (), s32[]{:S(2)}) async-start(), calls=%async_computation.3 | async-start | bytes 1474560 | tf_op jit(solution)/shard_map/reduce_scatter | solution.py:73
  382.0 33.3 %copy-start.2 = (s32[32]{0:T(128)S(1)}, s32[32]{0:T(128)}, u32[]{:S(2)}) copy-start(s32[32]{0:T(128)} %param.12) | copy-start | bytes 388
  382.0 44.3 %slice-start = ((s8[6291456]{0:T(1024)(128)(4,1)}), s8[2097152]{0:T(1024)(128)(4,1)S(1)}, s32[]{:S(2)}) async-start(s8[6291456]{0:T(1024)(128)(4,1)} %bitcast.29), calls=%async_computation.4 | async-start | bytes 4194304
  415.3 11.1 %copy-start.3 = (f32[32]{0:T(128)}, f32[32]{0:T(128)S(1)}, u32[]{:S(2)}) copy-start(f32[32]{0:T(128)S(1)} %maximum_divide_fusion) | copy-start | bytes 388
  415.3 11.0 %slice-start.1 = ((s8[6291456]{0:T(1024)(128)(4,1)}), s8[4194304]{0:T(1024)(128)(4,1)S(1)}, s32[]{:S(2)}) async-start(s8[6291456]{0:T(1024)(128)(4,1)} %bitcast.29), calls=%async_computation.5 | async-start | bytes 8388608
  434.5 26.4 %copy-start = (f32[192,768]{1,0:T(8,128)S(1)}, f32[192,768]{1,0:T(8,128)}, u32[]{:S(2)}) copy-start(f32[192,768]{1,0:T(8,128)} %param.13) | copy-start | bytes 1769476
  434.5 26.4 %copy-start.1 = (f32[192,768]{1,0:T(8,128)S(1)}, f32[192,768]{1,0:T(8,128)}, u32[]{:S(2)}) copy-start(f32[192,768]{1,0:T(8,128)} %param.14) | copy-start | bytes 1769476
Sparse Core Ops, SparseCore 0:
  10.2 178.8 all-gather.4
  191.2 174.2 all-gather.2
  437.9 22.8 reduce-scatter.3
where the time goes:
time: 470 us
  waiting for transfers between devices  353 us (75%)
  matrix products  77.6 us (17%)
  blocking collectives  18.7 us (4%)
  between operations  13.8 us (3%)
    all_gather x1, waiting for transfers between devices, local(): lax.all_gather(output_cot, 'mp', axis=0, tiled=True)  169 us
    all_gather x1, waiting for transfers between devices, local(): lax.all_gather(layer_input, 'mp', axis=0, tiled=True)  160 us
    reduce_scatter x1, waiting for transfers between devices, local(): lax.psum_scatter(gradient_rows(input_full, outcot_full, scaled_cot, scale...  23 us
    psum x1, blocking collectives, local(): squares = lax.psum(partial_squares, 'mp')  18.7 us
    dot_general x1, matrix products, squared_norms(): jnp.einsum('esd,etd->est', outcot_rows, outcot_rows, preferred_element_ty...  16.7 us
    dot_general x1, matrix products, squared_norms(): jnp.einsum('esd,etd->est', input_rows, input_rows, preferred_element_type...  16.5 us
    dot_general x1, matrix products, squared_norms(): jnp.einsum('efs,eft->est', cot_rows, cot_rows, preferred_element_type=jnp...  14.5 us
    dot_general x1, matrix products, gradient_rows(): lax.dot_general(outcot_rows, hid_rows, contract, preferred_element_type=j...  11 us
  transfers between devices with their start and end apart: 3, of which 3 were waited for; matrix products, arithmetic and copies ran while one was open for 6% of the time, Pallas kernels for 0%

commit v1 on v0

--- a/solution.py
+++ b/solution.py
@@ -63,7 +63,9 @@
     local_examples = lengths.shape[0]
     input_full, outcot_full = (
         lax.all_gather(layer_input, "mp", axis=0, tiled=True),
-        lax.all_gather(output_cot, "mp", axis=0, tiled=True),
+        jnp.concatenate(
+            lax.all_to_all(jnp.stack([output_cot] * lax.axis_size("mp")), "mp", 0, 0), axis=0
+        ),
     )
     token_mask, cot_masked, hid_masked = masked_rows(lengths, hidden_cot, hidden_act)
     partial_squares = squared_norms(input_full, outcot_full, cot_masked, hid_masked)

time: 470 us -> 569 us (1.21)
  waiting for transfers between devices: 353 us -> 437 us
  local copies, waits for them, and re-layouts: 3.2 us -> 10.7 us
  starting transfers between devices: 0.11 us -> 7.49 us
    all_to_all x0 -> x1, waiting for transfers between devices: none -> 413 us  [local(): lax.all_to_all(jnp.stack([output_cot] * lax.axis_size('mp')), 'mp', 0, 0)]
    all_gather x1 -> x0, waiting for transfers between devices: 169 us -> none  [local(): lax.all_gather(output_cot, 'mp', axis=0, tiled=True)]
    all_gather x1, waiting for transfers between devices: 160 us -> 0.01 us  [local(): lax.all_gather(layer_input, 'mp', axis=0, tiled=True)]
    another operation x0 -> x1, local copies, waits for them, and re-layouts: none -> 7.49 us  [local(): jnp.stack([output_cot] * lax.axis_size('mp'))]
    all_to_all x0 -> x1, starting transfers between devices: none -> 7.41 us  [local(): lax.all_to_all(jnp.stack([output_cot] * lax.axis_size('mp')), 'mp', 0, 0)]
  transfers between devices with their start and end apart: 3 -> 3, of which waited for: 3 -> 2; matrix products, arithmetic and copies ran while one was open for 6% -> 5% of each run, Pallas kernels for 0% -> 0%
where the time goes in v1:
time: 569 us
  waiting for transfers between devices  437 us (77%)
  matrix products  77.6 us (14%)
  blocking collectives  19.5 us (3%)
  between operations  14.1 us (2%)
  local copies, waits for them, and re-layouts  10.7 us (2%)
  starting transfers between devices  7.49 us (1%)
    all_to_all x1, waiting for transfers between devices, local(): lax.all_to_all(jnp.stack([output_cot] * lax.axis_size('mp')), 'mp', 0, 0)  413 us
    reduce_scatter x1, waiting for transfers between devices, local(): lax.psum_scatter(gradient_rows(input_full, outcot_full, scaled_cot, scale...  23 us
    psum x1, blocking collectives, local(): squares = lax.psum(partial_squares, 'mp')  19.5 us
    dot_general x1, matrix products, squared_norms(): jnp.einsum('esd,etd->est', input_rows, input_rows, preferred_element_type...  16.6 us
    dot_general x1, matrix products, squared_norms(): jnp.einsum('esd,etd->est', outcot_rows, outcot_rows, preferred_element_ty...  16.5 us
    dot_general x1, matrix products, squared_norms(): jnp.einsum('efs,eft->est', cot_rows, cot_rows, preferred_element_type=jnp...  14.6 us
  transfers between devices with their start and end apart: 3, of which 2 were waited for; matrix products, arithmetic and copies ran while one was open for 5% of the time, Pallas kernels for 0%

profile of v1, /device:TPU:0, one launch (start us, length us, event | category | flops | bytes accessed | tf_op | source)
XLA Modules:
  0.0 569.2 jit_solution(17270225616599837397)
XLA Ops:
  7.2 7.5 %stack.11 = bf16[8,4,256,768]{3,2,1,0:T(8,128)(2,1)} broadcast(bf16[4,256,768]{2,1,0:T(8,128)(2,1)} %param.9), dimensions={1,2,3} | broadcast | bytes 14155776 | tf_op jit(solution)/shard_map/stack | solution.py:67
  14.7 0.0 copy-start.2
  14.7 7.4 %all-to-all-start = ((bf16[8,4,256,768]{3,2,1,0:T(8,128)(2,1)}), bf16[8,4,256,768]{3,2,1,0:T(8,128)(2,1)}, u32[]{:S(2)}, u32[]{:S(2)}) async-start(bf16[8,4,256,768]{3,2,1,0:T(8,128)(2,1)} %stack.11), calls=%async_computation | async-start | bytes 25165824 | tf_op jit(solution)/shard_map/all_to_all | solution.py:67
  22.1 0.0 all-gather.2.cloned.1.call-start
  22.1 0.7 all-gather.2.cloned.1.call-update
  22.8 0.0 reduce-scatter.4.cloned.1.call-start
  22.8 0.0 copy-done.2
  22.9 0.1 fusion.40
  22.9 10.8 %fusion.6 = f32[32,256,256]{2,1,0:T(8,128)} fusion(bf16[32,384,256]{2,1,0:T(8,128)(2,1)} %param.10, f32[32,256]{1,0:T(8,128)S(1)} %fusion.40), kind=kOutput, calls=%fused_computation.10 | convolution fusion | flops 1620049920 | bytes 14712832 | tf_op jit(solution)/shard_map/efs,eft->est/dot_general | solution.py:26
  33.8 413.2 %all-to-all-done = bf16[8,4,256,768]{3,2,1,0:T(8,128)(2,1)} async-done(((bf16[8,4,256,768]{3,2,1,0:T(8,128)(2,1)}), bf16[8,4,256,768]{3,2,1,0:T(8,128)(2,1)}, u32[]{:S(2)}, u32[]{:S(2)}) %all-to-all-start) | async-done | bytes 12582944 | tf_op jit(solution)/shard_map/all_to_all | solution.py:67
  447.0 16.5 %fusion.44 = f32[32,256,256]{2,1,0:T(8,128)} fusion(bf16[32,256,768]{2,1,0:T(8,128)(2,1)} %bitcast), kind=kOutput, calls=%fused_computation.36 | convolution fusion | flops 3221225472 | bytes 20971520 | tf_op jit(solution)/shard_map/esd,etd->est/dot_general | solution.py:23
  463.5 0.0 all-gather.2.cloned.1.call-done
  463.5 16.6 %fusion.43 = f32[32,256,256]{2,1,0:T(8,128)} fusion(bf16[32,256,768]{2,1,0:T(8,128)(2,1)} %all-gather.2.cloned.1.call-done), kind=kOutput, calls=%fused_computation.35 | convolution fusion | flops 3221225472 | bytes 20971520 | tf_op jit(solution)/shard_map/esd,etd->est/dot_general | solution.py:19
  480.1 14.6 %add_reduce_fusion = f32[32]{0:T(128)S(1)} fusion(f32[32,256,256]{2,1,0:T(8,128)} %fusion.44, f32[32,256,256]{2,1,0:T(8,128)} %fusion.6, f32[32,256,256]{2,1,0:T(8,128)} %fusion.43, bf16[32,384,256]{2,1,0:T(8,128)(2,1)} %param.11, f32[32,256]{1,0:T(8,128)S(1)} %fusion.40), kind=kOutput, calls=%fused_computation.8 | convolution fusion | flops 1628438528 | bytes 31490176 | tf_op jit(solution)/shard_map/efs,eft->est/dot_general | solution.py:22
  494.7 19.5 %psum.7 = f32[32]{0:T(128)S(1)} all-reduce(f32[32]{0:T(128)S(1)} %add_reduce_fusion), channel_id=1, replica_groups=mesh['dp'=4,'mp'=8] {'mp'}, use_global_device_ids=true, to_apply=%region_1.0 | all-reduce | flops 32 | bytes 256 | tf_op jit(solution)/shard_map/psum | solution.py:72
  514.2 0.1 fusion.39
  514.3 11.0 %fusion.33 = bf16[768,384,1]{0,1,2:T(8,128)(2,1)S(1)} fusion(bf16[32,256,768]{2,1,0:T(8,128)(2,1)} %bitcast, bf16[32,384,256]{2,1,0:T(8,128)(2,1)} %param.10, f32[32,256]{1,0:T(8,128)S(1)} %fusion.39), kind=kOutput, calls=%fused_computation.22 | convolution fusion | flops 4841570304 | bytes 19496960 | tf_op jit(solution)/shard_map/dot_general | solution.py:53
  525.3 0.0 copy-done.3
  525.3 0.0 slice-done
  525.3 0.0 slice-done.1
  525.3 8.1 %fusion.30 = bf16[768,384,1]{0,1,2:T(8,128)(2,1)S(1)} fusion(bf16[32,256,768]{2,1,0:T(8,128)(2,1)} %all-gather.2.cloned.1.call-done, bf16[32,384,256]{2,1,0:T(8,128)(2,1)S(1)} %bitcast.31, f32[32,256]{1,0:T(8,128)S(1)} %fusion.39), kind=kOutput, calls=%fused_computation.21 | convolution fusion | flops 4841570304 | bytes 19496960 | tf_op jit(solution)/shard_map/dot_general | solution.py:52
  533.4 0.0 copy-start
  533.4 0.0 copy-start.1
  533.4 0.1 pad_maximum_fusion
  533.6 1.2 copy.36
  534.8 0.5 convert_element_type.41
  535.3 1.5 copy.40
  536.7 0.0 reduce-scatter.4.cloned.1.call-update
  536.8 23.0 %reduce-scatter.4.cloned.1.call-done = bf16[192,768]{1,0:T(8,128)(2,1)} async-done(((bf16[768,768]{1,0:T(8,128)(2,1)}), bf16[192,768]{1,0:T(8,128)(2,1)}) %reduce-scatter.4.cloned.1.call-update) | async-done | bytes 294928 | tf_op jit(solution)/shard_map/reduce_scatter | solution.py:75
  559.7 0.0 copy-done
  559.7 0.0 copy-done.1
  559.7 2.7 multiply_subtract_fusion
  (5 shorter events, 0.0 us)
Async XLA Ops:
  14.7 8.2 %copy-start.2 = (s32[32]{0:T(128)S(1)}, s32[32]{0:T(128)}, u32[]{:S(2)}) copy-start(s32[32]{0:T(128)} %param.12) | copy-start | bytes 388
  14.7 432.3 %all-to-all-start = ((bf16[8,4,256,768]{3,2,1,0:T(8,128)(2,1)}), bf16[8,4,256,768]{3,2,1,0:T(8,128)(2,1)}, u32[]{:S(2)}, u32[]{:S(2)}) async-start(bf16[8,4,256,768]{3,2,1,0:T(8,128)(2,1)} %stack.11), calls=%async_computation | async-start | bytes 25165824 | tf_op jit(solution)/shard_map/all_to_all | solution.py:67
  22.1 441.4 %all-gather.2.cloned.1.call-start = ((), (), s32[]{:S(2)}) async-start(), calls=%async_computation.2 | async-start | bytes 14155776 | tf_op jit(solution)/shard_map/all_gather | solution.py:65
  22.8 536.9 %reduce-scatter.4.cloned.1.call-start = ((), (), s32[]{:S(2)}) async-start(), calls=%async_computation.3 | async-start | bytes 1474560 | tf_op jit(solution)/shard_map/reduce_scatter | solution.py:75
  480.1 45.2 %slice-start = ((s8[6291456]{0:T(1024)(128)(4,1)}), s8[2097152]{0:T(1024)(128)(4,1)S(1)}, s32[]{:S(2)}) async-start(s8[6291456]{0:T(1024)(128)(4,1)} %bitcast.30), calls=%async_computation.4 | async-start | bytes 4194304
  514.2 11.1 %copy-start.3 = (f32[32]{0:T(128)}, f32[32]{0:T(128)S(1)}, u32[]{:S(2)}) copy-start(f32[32]{0:T(128)S(1)} %maximum_divide_fusion) | copy-start | bytes 388
  514.3 11.0 %slice-start.1 = ((s8[6291456]{0:T(1024)(128)(4,1)}), s8[4194304]{0:T(1024)(128)(4,1)S(1)}, s32[]{:S(2)}) async-start(s8[6291456]{0:T(1024)(128)(4,1)} %bitcast.30), calls=%async_computation.5 | async-start | bytes 8388608
  533.4 26.3 %copy-start = (f32[192,768]{1,0:T(8,128)S(1)}, f32[192,768]{1,0:T(8,128)}, u32[]{:S(2)}) copy-start(f32[192,768]{1,0:T(8,128)} %param.13) | copy-start | bytes 1769476
  533.4 26.3 %copy-start.1 = (f32[192,768]{1,0:T(8,128)S(1)}, f32[192,768]{1,0:T(8,128)}, u32[]{:S(2)}) copy-start(f32[192,768]{1,0:T(8,128)} %param.14) | copy-start | bytes 1769476
Sparse Core Ops, SparseCore 0:
  25.1 406.3 all-gather.1
  536.9 22.8 reduce-scatter.3
